TPU v7x, 32 devices: a whole 2x2x4 slice. The times are simulated.
32 devices in a mesh: slab: 16 (over z, x, core), chan: 2 (over y).
Axes of the slice: x: 2, y: 2, z: 4, core: 2. Of those that a mesh axis runs over, the one named last changes fastest.
Arguments:
- species: int32 [4096], P('slab'), may hold values from 0 to 4
- atom_count: int32 [16], P('slab'), may hold values from 192 to 256, as said below
- halo_index: int32 [16, 2, 128], P('slab'), may hold values from 0 to 255, as said below
- edge_count: int32 [16, 2], P('slab'), may hold values from 512 to 12288, as said below
- inner_edges: int32 [2, 196608], P(None, 'slab'), may hold values from 0 to 255, as said below
- outer_edges: int32 [2, 65536], P(None, 'slab'), may hold values from 0 to 255, as said below
- inner_vec: float32 [3, 196608], P(None, 'slab'), may hold values from -4.8 to 4.8, as said below
- outer_vec: float32 [3, 65536], P(None, 'slab'), may hold values from -4.8 to 4.8, as said below
- embed_table: bfloat16 [64, 5], replicated, may hold values from -6 to 6
- radial_in: bfloat16 [2, 64, 8], replicated, may hold values from -2 to 2
- radial_mid: bfloat16 [2, 64, 64], replicated, may hold values from -0.75 to 0.75
- radial_out: bfloat16 [2, 10, 64, 64], P(None, None, 'chan'), may hold values from -0.75 to 0.75
- mix_in: bfloat16 [2, 3, 64, 64], P(None, None, 'chan'), may hold values from -0.75 to 0.75
- mix_scalar: bfloat16 [2, 192, 64], replicated, may hold values from -0.75 to 0.75
- mix_irrep: bfloat16 [2, 2, 64, 64], replicated, may hold values from -0.75 to 0.75
- readout: float32 [64], replicated, may hold values from -0.75 to 0.75
- species_energy: float32 [5], replicated, may hold values from -6 to -2
Outputs:
- node_state: float32 [9, 64, 4096], P(None, None, 'slab')
- atom_energy: float32 [4096], P('slab')
- mean_energy: float32 [], replicated
Inputs may be any that keep to these rules, and one draw needn't show every extreme that they name: `atom_count`: each slab holds between 192 and 256 live atoms (rounded down), live slots first; some slab holds exactly 256. `halo_index`: every entry names a live atom of its own slab. `edge_count`: column 0 lies between 1536 and 12288, column 1 between 512 and 4096 (rounded down); live slots come first in each list; each column reaches its most in some slab. `inner_edges`: both rows name live atoms of the same slab, in every slot. `outer_edges`: row 0 lies below 256; row 1 names a live atom of the slab, in every slot. `inner_vec`: every displacement is shorter than 4.8; nearly all are 0.9 or longer, and a rare few are shorter. `outer_vec`: every displacement is shorter than 4.8; nearly all are 0.9 or longer, and a rare few are shorter.
All inputs are finite; a program needn't handle non-finite values.
Results may differ from a plain program's by a relative error of at most 0.00045.
Values may be sent and summed in bfloat16 or wider, within the bound.
A program may use at most 64 MiB of HBM per device.

v0:
```python
import functools
import math

import jax
import jax.numpy as jnp
from jax import lax
from jax.experimental import pallas as pl
from jax.experimental.pallas import tpu as pltpu
from jax.sharding import PartitionSpec as P

cutoff = 5.0
neighbour_norm = 1.0 / math.sqrt(48.0)
root_three = math.sqrt(3.0)
half_root = 0.5 * math.sqrt(3.0)
BLOCK = 2048
WIDE = 4096
TALL, LANES = 16, 128
GROUPS = ((0, 1), (1, 4), (4, 9))
f32 = jnp.float32
bf16 = jnp.bfloat16


def dot(a, b):
    return jnp.dot(a, b, preferred_element_type=f32)


def dot_nt(a, b):
    return lax.dot_general(a, b, (((1,), (1,)), ((), ())), preferred_element_type=f32)


def sigmoid(v):
    return 0.5 * jnp.tanh(0.5 * v) + 0.5


def silu(v):
    half = 0.5 * v
    return half * jnp.tanh(half) + half


def number_rows(rows):
    return lax.broadcasted_iota(jnp.int32, (rows, LANES), 0).astype(f32).astype(bf16)


def onehot_tiles(index, number_ref):
    rows = number_ref.shape[0]
    tiles = []
    for low in range(0, index.shape[1], LANES):
        part = index[:, low : low + LANES].astype(f32)
        part = jnp.broadcast_to(part, (rows, LANES)).astype(bf16)
        tiles.append(jnp.where(number_ref[...] == part, 1.0, 0.0).astype(bf16))
    return jnp.concatenate(tiles, axis=1)


def onehot_rows(index, rows):
    slots = lax.broadcasted_iota(jnp.int32, (rows, index.shape[1]), 0)
    return jnp.where(slots == index, 1.0, 0.0).astype(bf16)


def turned(matrix):
    return matrix.astype(f32).T.astype(bf16)


def initial(embed_ref, species_row):
    return dot(turned(embed_ref[...]), onehot_rows(species_row, embed_ref.shape[0]))


def unit(vec):
    x, y, z = vec[0:1], vec[1:2], vec[2:3]
    squared = x * x + y * y + z * z
    inverse = lax.rsqrt(squared + 0.25)
    return squared, inverse, x * inverse, y * inverse, z * inverse


def bessel_rows(squared, inverse, orders):
    length = jnp.sqrt(squared)
    fraction = jnp.minimum(length * (1.0 / cutoff), 1.0)
    cube = fraction * fraction * fraction
    sixth = cube * cube
    envelope = 1.0 - sixth * (28.0 - fraction * (48.0 - 21.0 * fraction))
    half = length * (0.5 * math.pi / cutoff)
    h2 = half * half
    sine = 1.0
    cosine = 1.0
    for order in range(12, 0, -2):
        sine = 1.0 - sine * h2 * (1.0 / ((order + 1) * order))
        cosine = 1.0 - cosine * h2 * (1.0 / (order * (order - 1)))
    sine = sine * half
    twice_cos = 2.0 - 4.0 * sine * sine
    first = 2.0 * sine * cosine
    scale = math.sqrt(2.0 / cutoff) * inverse * envelope
    before, now = jnp.zeros_like(first), first * scale
    rows = []
    for _ in range(orders):
        rows.append(now)
        before, now = now, twice_cos * now - before
    return jnp.concatenate(rows, axis=0)


def harmonics(x, y, z):
    return [
        root_three * x * y,
        root_three * y * z,
        0.5 * (2.0 * z * z - x * x - y * y),
        root_three * x * z,
        half_root * (x * x - y * y),
    ]


def radial(entry, mid, basis):
    hidden = silu(dot(entry, basis)).astype(bf16)
    return silu(dot(mid, hidden)).astype(bf16)


mesh_ids = pl.DeviceIdType.MESH


def greet(peers):
    barrier = pltpu.get_barrier_semaphore()
    for peer in peers:
        pl.semaphore_signal(barrier, inc=1, device_id=peer, device_id_type=mesh_ids)
    pl.semaphore_wait(barrier, len(peers))


def others(axis, total):
    me = lax.axis_index(axis)
    return [{axis: lax.rem(me + step, total)} for step in range(1, total)]


def beside(total):
    me = lax.axis_index("slab")
    return {"slab": lax.rem(me + total - 1, total)}, {"slab": lax.rem(me + 1, total)}


def remote(src, dst, send_sem, recv_sem, peer):
    return pltpu.make_async_remote_copy(
        src_ref=src,
        dst_ref=dst,
        send_sem=send_sem,
        recv_sem=recv_sem,
        device_id=peer,
        device_id_type=mesh_ids,
    )


def send_halo(send_ref, land_ref, send_sem, recv_sem, total):
    copies = [
        remote(send_ref.at[side], land_ref.at[1 - side], send_sem.at[side], recv_sem.at[side], peer)
        for side, peer in enumerate(beside(total))
    ]
    for copy in copies:
        copy.start()
    return copies


def exchange(agg_ref, all_ref, send_sem, recv_sem, total):
    part = agg_ref.shape[0] // 9
    me = lax.axis_index("chan")
    peers = others("chan", total)
    copies = []
    for k, (low, high) in enumerate(GROUPS):
        span = slice(low * part, high * part)
        for i, peer in enumerate(peers):
            copies.append(
                remote(agg_ref.at[span], all_ref.at[me, span], send_sem.at[i, k], recv_sem.at[i, k], peer)
            )
    for copy in copies:
        copy.start()
    all_ref[me] = agg_ref[...]

    def component(k):
        for group, (low, high) in enumerate(GROUPS):
            if k == low:
                for copy in copies[group * len(peers) : (group + 1) * len(peers)]:
                    copy.wait_recv()
        span = slice(k * part, (k + 1) * part)
        return jnp.concatenate([all_ref[i, span] for i in range(total)], axis=0)

    return copies, component


class Updates:
    def __init__(self, component, scalar, irrep_ref, layer):
        self.component, self.layer, self.irrep = component, layer, irrep_ref
        chans = irrep_ref.shape[2]
        y = dot(scalar, component(0))
        self.scalar = silu(y[:chans])
        self.gates = sigmoid(y[chans : 2 * chans]), sigmoid(y[2 * chans :])

    def __getitem__(self, k):
        if k == 0:
            return self.scalar
        kind = 0 if k < 4 else 1
        return self.gates[kind] * dot(self.irrep[self.layer, kind], self.component(k))


def tall(row):
    return jnp.broadcast_to(row, (TALL, LANES)).astype(bf16)


def kernel(
    slabs,
    parts,
    block,
    wide,
    live_ref,
    count_ref,
    energy_ref,
    species_ref,
    halo_ref,
    inner_edges_ref,
    outer_edges_ref,
    inner_vec_ref,
    outer_vec_ref,
    embed_ref,
    radial_in_ref,
    radial_mid_ref,
    radial_out_ref,
    mix_ref,
    scalar_ref,
    irrep_ref,
    readout_ref,
    state_ref,
    atom_ref,
    mean_ref,
    acc_ref,
    mess_ref,
    source_ref,
    weight_ref,
    basis_ref,
    geo_ref,
    hidden_ref,
    table_ref,
    halo_table_ref,
    first_table_ref,
    paths_ref,
    number_ref,
    agg_ref,
    all_ref,
    send_ref,
    land_ref,
    kind_send_ref,
    kind_land_ref,
    energies_ref,
    kind_send,
    kind_recv,
    agg_send,
    agg_recv,
    halo_send,
    halo_recv,
    energy_send,
    energy_recv,
):
    part = mix_ref.shape[2]
    chans, atoms = state_ref.shape[1:]
    inner_total = inner_edges_ref.shape[1]
    held = halo_ref.shape[1]
    greet(others("chan", parts) + others("slab", slabs))

    values = jnp.broadcast_to(species_ref[...].astype(f32), (16, atoms)).astype(bf16)
    for side in range(2):
        kind_send_ref[side] = dot(values, onehot_rows(halo_ref[side : side + 1], atoms))[0:8]
    kind_copies = send_halo(kind_send_ref, kind_land_ref, kind_send, kind_recv, slabs)

    number_ref[...] = number_rows(atoms)
    start = initial(embed_ref, species_ref[...])
    first_table_ref[0] = dot(mix_ref[0, 0], start.astype(bf16)).astype(bf16)
    for k, path in enumerate((0, 3, 7)):
        paths_ref[k * part : (k + 1) * part] = radial_out_ref[0, path]
    acc_ref[...] = jnp.zeros_like(acc_ref)
    entry = turned(radial_in_ref[0])
    lists = (
        (inner_edges_ref, inner_vec_ref, 0, live_ref[0, 0]),
        (outer_edges_ref, outer_vec_ref, inner_total, live_ref[0, 1]),
    )

    def scatter(edges_ref, span, offset, live):
        lanes = lax.broadcasted_iota(jnp.int32, (1, block), 1) + offset
        target = jnp.where(lanes < live, edges_ref[1:2, span], -1)
        acc_ref[...] += dot_nt(mess_ref[...], onehot_tiles(target, number_ref))

    def first(which, step):
        edges_ref, vec_ref, base, live = lists[which]
        offset = pl.multiple_of(step * block, block)
        span = pl.ds(offset, block)
        place = pl.ds(pl.multiple_of(base + step * block, block), block)
        gathered = dot(first_table_ref[which], onehot_tiles(edges_ref[0:1, span], number_ref))
        squared, inverse, x, y, z = unit(vec_ref[:, span])
        basis = bessel_rows(squared, inverse, radial_in_ref.shape[1]).astype(bf16)
        basis_ref[:, place] = basis
        rows = [x, y, z] + harmonics(x, y, z)
        geo_ref[:, place] = jnp.concatenate(rows, axis=0)
        weights = dot(paths_ref[...], radial(entry, radial_mid_ref[0], basis))
        for lane in range(0, block, LANES):
            cols = slice(lane, lane + LANES)
            around = [tall(row[:, cols]) for row in rows]
            for low in range(0, part, TALL):

                def lead(k):
                    at = slice(k * part + low, k * part + low + TALL)
                    return (weights[at, cols] * gathered[low : low + TALL, cols]).astype(bf16)

                def put(k, value):
                    mess_ref[k * part + low : k * part + low + TALL, cols] = value

                put(0, lead(0))
                for k, (low_k, high_k) in enumerate(GROUPS[1:]):
                    value = lead(1 + k)
                    for j in range(low_k, high_k):
                        put(j, value * around[j - 1])
        scatter(edges_ref, span, offset, live)

    def second(which, step):
        edges_ref, _, base, live = lists[which]
        offset = pl.multiple_of(step * block, block)
        span = pl.ds(offset, block)
        place = pl.ds(pl.multiple_of(base + step * block, block), block)
        features_ref = (table_ref, halo_table_ref)[which]
        source_ref[...] = dot(features_ref[...], onehot_tiles(edges_ref[0:1, span], number_ref)).astype(bf16)
        weight_ref[...] = dot(radial_out, hidden_ref[:, place]).astype(bf16)
        geo = geo_ref[:, place]
        for lane in range(0, block, LANES):
            cols = slice(lane, lane + LANES)
            rows = [geo[k : k + 1, cols] for k in range(8)]
            x, y, z, *q = [tall(row) for row in rows]
            hx, hy, hz = [tall(half_root * row) for row in rows[:3]]
            for low in range(0, part, TALL):

                def at(ref, k):
                    return ref[k * part + low : k * part + low + TALL, cols]

                def put(k, value):
                    mess_ref[k * part + low : k * part + low + TALL, cols] = value

                s = at(source_ref, 0)
                v = [at(source_ref, k) for k in (1, 2, 3)]
                t = [at(source_ref, k) for k in (4, 5, 6, 7, 8)]
                along = v[0] * x + v[1] * y + v[2] * z
                tq = t[0] * q[0] + t[1] * q[1] + t[2] * q[2] + t[3] * q[3] + t[4] * q[4]
                put(0, at(weight_ref, 0) * s + at(weight_ref, 1) * tq + at(weight_ref, 2) * along)
                ws = at(weight_ref, 3) * s
                w4, w5, w6 = at(weight_ref, 4), at(weight_ref, 5), at(weight_ref, 6)
                cross = [
                    v[1] * z - v[2] * y,
                    v[2] * x - v[0] * z,
                    v[0] * y - v[1] * x,
                ]
                t3 = 0.5 * t[2]
                grad = [
                    hy * t[0] - x * t3 + hz * t[3] + hx * t[4],
                    hx * t[0] + hz * t[1] - y * t3 - hy * t[4],
                    hy * t[1] + z * t[2] + hx * t[3],
                ]
                for k, side in enumerate((x, y, z)):
                    put(1 + k, ws * side + w4 * v[k] + w5 * cross[k] + w6 * grad[k])
                ws = at(weight_ref, 7) * s
                w8, w9 = at(weight_ref, 8), at(weight_ref, 9)
                sym = [
                    hy * v[0] + hx * v[1],
                    hz * v[1] + hy * v[2],
                    1.5 * v[2] * z - 0.5 * along,
                    hz * v[0] + hx * v[2],
                    hx * v[0] - hy * v[1],
                ]
                for k in range(5):
                    put(4 + k, ws * q[k] + w8 * t[k] + w9 * sym[k])
        scatter(edges_ref, span, offset, live)

    def sweep(visit, which):
        def body(step, carry):
            visit(which, step)
            return carry

        lax.fori_loop(0, lists[which][0].shape[1] // block, body, 0)

    sweep(first, 0)
    for copy in kind_copies:
        copy.wait()
    kinds = jnp.concatenate([kind_land_ref[0, 0:1], kind_land_ref[1, 0:1]], axis=1).astype(jnp.int32)
    first_table_ref[1] = dot(mix_ref[0, 0], initial(embed_ref, kinds).astype(bf16)).astype(bf16)
    sweep(first, 1)
    agg_ref[0] = (acc_ref[...] * neighbour_norm).astype(bf16)
    copies, component = exchange(agg_ref.at[0], all_ref.at[0], agg_send.at[0], agg_recv.at[0], parts)
    acc_ref[...] = jnp.zeros_like(acc_ref)
    entry_next = turned(radial_in_ref[1])

    def prepare(step, carry):
        span = pl.ds(pl.multiple_of(step * wide, wide), wide)
        hidden_ref[:, span] = radial(entry_next, radial_mid_ref[1], basis_ref[:, span])
        return carry

    lax.fori_loop(0, basis_ref.shape[1] // wide, prepare, 0)
    picks = jnp.concatenate([onehot_rows(halo_ref[side : side + 1], atoms) for side in range(2)], axis=1)
    outs = Updates(component, turned(scalar_ref[0]), irrep_ref, 0)
    for k in range(9):
        out = outs[k]
        if k == 0:
            out += start
        state_ref[k] = out
        which = 0 if k == 0 else (1 if k < 4 else 2)
        span = slice(k * part, (k + 1) * part)
        mixed = dot(mix_ref[1, which], out.astype(bf16)).astype(bf16)
        table_ref[span] = mixed
        picked = dot(mixed, picks).astype(bf16)
        for side in range(2):
            send_ref[side, span] = picked[:, side * held : (side + 1) * held]
    for copy in copies:
        copy.wait_send()
    halo_copies = send_halo(send_ref, land_ref, halo_send, halo_recv, slabs)

    paths, _, breadth = radial_out_ref.shape[1:]
    radial_out = radial_out_ref[1].reshape(paths * part, breadth)
    sweep(second, 0)
    for copy in halo_copies:
        copy.wait()
    for side in range(2):
        halo_table_ref[:, side * held : (side + 1) * held] = land_ref[side]
    sweep(second, 1)
    agg_ref[1] = (acc_ref[...] * neighbour_norm).astype(bf16)
    copies, component = exchange(agg_ref.at[1], all_ref.at[1], agg_send.at[1], agg_recv.at[1], parts)
    lines = lax.broadcasted_iota(jnp.int32, (chans, chans), 0)
    across = lax.broadcasted_iota(jnp.int32, (chans, chans), 1)
    readout = jnp.sum(jnp.where(lines == across, readout_ref[...], 0.0), axis=1, keepdims=True)
    own = jnp.zeros((1, atoms), f32)
    for kind in range(energy_ref.shape[0]):
        own = jnp.where(species_ref[...] == kind, energy_ref[kind], own)
    lanes = lax.broadcasted_iota(jnp.int32, (1, atoms), 1)
    outs = Updates(component, turned(scalar_ref[1]), irrep_ref, 1)
    out = state_ref[0] + outs[0]
    state_ref[0] = out
    total = jnp.sum(out * readout, axis=0, keepdims=True) + own
    total = jnp.where(lanes < count_ref[0], total, 0.0)
    me = lax.axis_index("slab")
    energies_ref[me] = jnp.broadcast_to(jnp.sum(total, axis=1, keepdims=True), energies_ref.shape[1:])
    atom_ref[...] = total
    sums = [
        remote(energies_ref.at[me], energies_ref.at[me], energy_send.at[i], energy_recv.at[i], peer)
        for i, peer in enumerate(others("slab", slabs))
    ]
    for copy in sums:
        copy.start()
    for k in range(1, 9):
        state_ref[k] = state_ref[k] + outs[k]
    for copy in copies:
        copy.wait_send()
    for copy in sums:
        copy.wait()
    mean_ref[...] = jnp.sum(energies_ref[...], axis=0)[0:1, 0:1] * (1.0 / (atoms * slabs))


vmem = pl.BlockSpec(memory_space=pltpu.VMEM)
smem = pl.BlockSpec(memory_space=pltpu.SMEM)


def local(
    species,
    atom_count,
    halo_index,
    edge_count,
    inner_edges,
    outer_edges,
    inner_vec,
    outer_vec,
    embed_table,
    radial_in,
    radial_mid,
    radial_out,
    mix_in,
    mix_scalar,
    mix_irrep,
    readout,
    species_energy,
):
    slabs = lax.axis_size("slab")
    parts = lax.axis_size("chan")
    atoms = species.shape[0]
    chans = embed_table.shape[0]
    part = mix_in.shape[2]
    breadth = radial_mid.shape[1]
    basis = radial_in.shape[2]
    paths = radial_out.shape[1]
    halo = halo_index[0]
    held = halo.shape[1]
    rows = 9 * part
    inner_total, outer_total = inner_edges.shape[1], outer_edges.shape[1]
    total = inner_total + outer_total
    shared = math.gcd(inner_total, outer_total)
    block = math.gcd(BLOCK, shared)
    wide = math.gcd(WIDE, shared)
    dma = pltpu.SemaphoreType.DMA
    node_state, atom_energy, mean_energy = pl.pallas_call(
        functools.partial(kernel, slabs, parts, block, wide),
        out_shape=(
            jax.ShapeDtypeStruct((9, chans, atoms), f32),
            jax.ShapeDtypeStruct((1, atoms), f32),
            jax.ShapeDtypeStruct((1, 1), f32),
        ),
        in_specs=[smem] * 3 + [vmem] * 14,
        out_specs=(vmem, vmem, vmem),
        scratch_shapes=[
            pltpu.VMEM((rows, atoms), f32),
            pltpu.VMEM((rows, block), bf16),
            pltpu.VMEM((rows, block), bf16),
            pltpu.VMEM((paths * part, block), bf16),
            pltpu.VMEM((basis, total), bf16),
            pltpu.VMEM((8, total), f32),
            pltpu.VMEM((breadth, total), bf16),
            pltpu.VMEM((rows, atoms), bf16),
            pltpu.VMEM((rows, 2 * held), bf16),
            pltpu.VMEM((2, part, atoms), bf16),
            pltpu.VMEM((3 * part, breadth), bf16),
            pltpu.VMEM((atoms, LANES), bf16),
            pltpu.VMEM((2, rows, atoms), bf16),
            pltpu.VMEM((2, parts, rows, atoms), bf16),
            pltpu.VMEM((2, rows, held), bf16),
            pltpu.VMEM((2, rows, held), bf16),
            pltpu.VMEM((2, 8, held), f32),
            pltpu.VMEM((2, 8, held), f32),
            pltpu.VMEM((slabs, 8, 128), f32),
            dma((2,)),
            dma((2,)),
            dma((2, parts - 1, 3)),
            dma((2, parts - 1, 3)),
            dma((2,)),
            dma((2,)),
            dma((slabs - 1,)),
            dma((slabs - 1,)),
        ],
        compiler_params=pltpu.CompilerParams(
            vmem_limit_bytes=60 * 1024 * 1024, collective_id=0, has_side_effects=True
        ),
        name="message_passing",
    )(
        edge_count,
        atom_count,
        species_energy,
        species[None, :],
        halo,
        inner_edges,
        outer_edges,
        inner_vec,
        outer_vec,
        embed_table.T,
        jnp.swapaxes(radial_in, 1, 2),
        radial_mid,
        radial_out,
        mix_in,
        jnp.swapaxes(mix_scalar, 1, 2),
        mix_irrep,
        readout[None, :],
    )
    return (node_state, atom_energy[0], mean_energy[0, 0])


def solution(mesh):
    return jax.shard_map(
        local,
        mesh=mesh,
        in_specs=(
            P("slab"),
            P("slab"),
            P("slab", None, None),
            P("slab", None),
            P(None, "slab"),
            P(None, "slab"),
            P(None, "slab"),
            P(None, "slab"),
            P(),
            P(),
            P(),
            P(None, None, "chan", None),
            P(None, None, "chan", None),
            P(),
            P(),
            P(),
            P(),
        ),
        out_specs=(P(None, None, "slab"), P("slab"), P()),
        check_vma=False,
    )
```

profile of v0, /device:TPU:0, one launch (start us, length us, event | category | flops | bytes accessed | tf_op | source)
XLA Modules:
  0.0 60.1 jit_solution(12727258004347792223)
XLA Ops:
  1.3 54.6 %message_passing.1 = (f32[9,64,256]{2,1,0:T(8,128)}, f32[1,256]{1,0:T(1,128)}, f32[1,1]{1,0:T(1,128)}) custom-call(s32[1,2]{1,0:T(1,128)} %live_ref.1, s32[1]{0:T(128)S(6)} %copy.23.count_ref, f32[5]{0:T(128)} %energy_ref.1, s32[1,256]{1,0:T(1,128)} %bitcast.11, s32[2,128]{1,0:T(2,128)} %bitcast.12, s32[2,12288]{1,0:T(2,128)} %inner_edges_ref.1, ...), custom_call_target="tpu_custom_call" | custom-call | tf_op jit(solution)/shard_map/message_passing/pallas_call | solution.py:490
  55.9 0.0 copy-start
  55.9 1.9 %copy.24 = f32[9,64,256]{2,1,0:T(8,128)} copy(f32[9,64,256]{2,1,0:T(8,128)} %get-tuple-element.12) | data formatting | bytes 1179648
  57.8 0.0 copy-done
  57.8 0.6 copy.25
Async XLA Ops:
  55.9 1.9 %copy-start = (f32[1,256]{1,0:T(1,128)S(1)}, f32[1,256]{1,0:T(1,128)}, u32[]{:S(2)}) copy-start(f32[1,256]{1,0:T(1,128)} %get-tuple-element.7) | copy-start | bytes 3076
where the time goes:
time: 60.3 us; the launch traced here: 60.1 us
  Pallas kernels  54.6 us (91%)
  between operations  3 us (5%)
  local copies, waits for them, and re-layouts  2.48 us (4%)
    pallas_call x1, Pallas kernels, local(): pl.pallas_call(functools.partial(kernel, slabs, parts, block, wide), out_...  54.6 us
    unnamed x4, local copies, waits for them, and re-layouts  2.48 us

commit v1 on v0

--- a/solution.py
+++ b/solution.py
@@ -43,11 +43,12 @@
 
 def onehot_tiles(index, number_ref):
     rows = number_ref.shape[0]
+    one, zero = jnp.ones((), bf16), jnp.zeros((), bf16)
     tiles = []
     for low in range(0, index.shape[1], LANES):
         part = index[:, low : low + LANES].astype(f32)
         part = jnp.broadcast_to(part, (rows, LANES)).astype(bf16)
-        tiles.append(jnp.where(number_ref[...] == part, 1.0, 0.0).astype(bf16))
+        tiles.append(jnp.where(number_ref[...] == part, one, zero))
     return jnp.concatenate(tiles, axis=1)
 
 
@@ -197,7 +198,27 @@
     return jnp.broadcast_to(row, (TALL, LANES)).astype(bf16)
 
 
-def kernel(
+def kernel(slabs, parts, block, wide, *refs):
+    radial_out_ref, irrep_ref, state_ref = refs[12], refs[15], refs[17]
+    _, paths, part, breadth = radial_out_ref.shape
+    atoms = state_ref.shape[2]
+    total = refs[5].shape[1] + refs[6].shape[1]
+    rows = 9 * part
+    pl.run_scoped(
+        functools.partial(program, slabs, parts, block, wide, *refs),
+        pltpu.VMEM((rows, block), bf16),
+        pltpu.VMEM((rows, block), bf16),
+        pltpu.VMEM((paths * part, block), bf16),
+        pltpu.VMEM((breadth, total), bf16),
+        pltpu.VMEM((rows, atoms), bf16),
+        pltpu.VMEM((rows, 2 * refs[4].shape[1]), bf16),
+        pltpu.VMEM((2, part, atoms), bf16),
+        pltpu.VMEM((3 * part, breadth), bf16),
+        pltpu.VMEM((atoms, LANES), bf16),
+    )
+
+
+def program(
     slabs,
     parts,
     block,
@@ -223,17 +244,8 @@
     atom_ref,
     mean_ref,
     acc_ref,
-    mess_ref,
-    source_ref,
-    weight_ref,
     basis_ref,
     geo_ref,
-    hidden_ref,
-    table_ref,
-    halo_table_ref,
-    first_table_ref,
-    paths_ref,
-    number_ref,
     agg_ref,
     all_ref,
     send_ref,
@@ -249,6 +261,15 @@
     halo_recv,
     energy_send,
     energy_recv,
+    mess_ref,
+    source_ref,
+    weight_ref,
+    hidden_ref,
+    table_ref,
+    halo_table_ref,
+    first_table_ref,
+    paths_ref,
+    number_ref,
 ):
     part = mix_ref.shape[2]
     chans, atoms = state_ref.shape[1:]
@@ -475,9 +496,7 @@
     atoms = species.shape[0]
     chans = embed_table.shape[0]
     part = mix_in.shape[2]
-    breadth = radial_mid.shape[1]
     basis = radial_in.shape[2]
-    paths = radial_out.shape[1]
     halo = halo_index[0]
     held = halo.shape[1]
     rows = 9 * part
@@ -498,17 +517,8 @@
         out_specs=(vmem, vmem, vmem),
         scratch_shapes=[
             pltpu.VMEM((rows, atoms), f32),
-            pltpu.VMEM((rows, block), bf16),
-            pltpu.VMEM((rows, block), bf16),
-            pltpu.VMEM((paths * part, block), bf16),
             pltpu.VMEM((basis, total), bf16),
             pltpu.VMEM((8, total), f32),
-            pltpu.VMEM((breadth, total), bf16),
-            pltpu.VMEM((rows, atoms), bf16),
-            pltpu.VMEM((rows, 2 * held), bf16),
-            pltpu.VMEM((2, part, atoms), bf16),
-            pltpu.VMEM((3 * part, breadth), bf16),
-            pltpu.VMEM((atoms, LANES), bf16),
             pltpu.VMEM((2, rows, atoms), bf16),
             pltpu.VMEM((2, parts, rows, atoms), bf16),
             pltpu.VMEM((2, rows, held), bf16),

time: 60.3 us -> 47.6 us (0.79)
  Pallas kernels: 54.6 us -> 41.9 us
    pallas_call x1, Pallas kernels: 54.6 us -> 41.9 us  [local(): pl.pallas_call(functools.partial(kernel, slabs, parts, block, wide), out_...]
where the time goes in v1:
time: 47.6 us; the launch traced here: 47.4 us
  Pallas kernels  41.9 us (88%)
  between operations  3 us (6%)
  local copies, waits for them, and re-layouts  2.48 us (5%)
    pallas_call x1, Pallas kernels, local(): pl.pallas_call(functools.partial(kernel, slabs, parts, block, wide), out_...  41.9 us
    unnamed x4, local copies, waits for them, and re-layouts  2.48 us

profile of v1, /device:TPU:0, one launch (start us, length us, event | category | flops | bytes accessed | tf_op | source)
XLA Modules:
  0.0 47.4 jit_solution(7699424045218715001)
XLA Ops:
  1.3 41.9 %message_passing.1 = (f32[9,64,256]{2,1,0:T(8,128)}, f32[1,256]{1,0:T(1,128)}, f32[1,1]{1,0:T(1,128)}) custom-call(s32[1,2]{1,0:T(1,128)} %refs_0_.1, s32[1]{0:T(128)S(6)} %copy.23.refs_1_, f32[5]{0:T(128)} %refs_2_.1, s32[1,256]{1,0:T(1,128)} %bitcast.11, s32[2,128]{1,0:T(2,128)} %bitcast.12, s32[2,12288]{1,0:T(2,128)} %refs_5_.1, s32[2,4096]{1,0:T(2,128)} %refs_6_.1, ...), custom_call_target="tpu_custom_call" | custom-call | tf_op jit(solution)/shard_map/message_passing/pallas_call | solution.py:509
  43.2 0.0 copy-start
  43.2 1.9 %copy.24 = f32[9,64,256]{2,1,0:T(8,128)} copy(f32[9,64,256]{2,1,0:T(8,128)} %get-tuple-element.12) | data formatting | bytes 1179648
  45.1 0.0 copy-done
  45.1 0.6 %copy.25 = f32[256]{0:T(256)} copy(f32[256]{0:T(256)S(1)} %bitcast.13) | data formatting | bytes 2048
Async XLA Ops:
  43.2 1.9 %copy-start = (f32[1,256]{1,0:T(1,128)S(1)}, f32[1,256]{1,0:T(1,128)}, u32[]{:S(2)}) copy-start(f32[1,256]{1,0:T(1,128)} %get-tuple-element.7) | copy-start | bytes 3076

commit v2 on v1

--- a/solution.py
+++ b/solution.py
@@ -12,9 +12,10 @@
 neighbour_norm = 1.0 / math.sqrt(48.0)
 root_three = math.sqrt(3.0)
 half_root = 0.5 * math.sqrt(3.0)
-BLOCK = 2048
-WIDE = 4096
+BLOCK, SUB = 4096, 512
+root_third = 1.0 / math.sqrt(3.0)
 TALL, LANES = 16, 128
+ARRAYS = 14
 GROUPS = ((0, 1), (1, 4), (4, 9))
 f32 = jnp.float32
 bf16 = jnp.bfloat16
@@ -66,7 +67,7 @@
 
 
 def unit(vec):
-    x, y, z = vec[0:1], vec[1:2], vec[2:3]
+    x, y, z = vec
     squared = x * x + y * y + z * z
     inverse = lax.rsqrt(squared + 0.25)
     return squared, inverse, x * inverse, y * inverse, z * inverse
@@ -94,7 +95,7 @@
     for _ in range(orders):
         rows.append(now)
         before, now = now, twice_cos * now - before
-    return jnp.concatenate(rows, axis=0)
+    return rows
 
 
 def harmonics(x, y, z):
@@ -198,20 +199,35 @@
     return jnp.broadcast_to(row, (TALL, LANES)).astype(bf16)
 
 
-def kernel(slabs, parts, block, wide, *refs):
-    radial_out_ref, irrep_ref, state_ref = refs[12], refs[15], refs[17]
+def staged(stages, total):
+    for time in range(total + len(stages) - 1):
+        for late in reversed(range(len(stages))):
+            if 0 <= time - late < total:
+                stages[late](time - late)
+
+
+def kernel(slabs, parts, block, *refs):
+    halo_ref, inner_edges_ref, outer_edges_ref = refs[4:7]
+    radial_out_ref, state_ref = refs[12], refs[17]
     _, paths, part, breadth = radial_out_ref.shape
     atoms = state_ref.shape[2]
-    total = refs[5].shape[1] + refs[6].shape[1]
+    total = inner_edges_ref.shape[1] + outer_edges_ref.shape[1]
     rows = 9 * part
+    *refs, sems = refs
+    held = refs[-ARRAYS:]
+    loads = [
+        pltpu.make_async_copy(source, target, sems.at[i])
+        for i, (source, target) in enumerate(zip(refs[3 : 3 + ARRAYS], held, strict=True))
+    ]
     pl.run_scoped(
-        functools.partial(program, slabs, parts, block, wide, *refs),
+        functools.partial(program, slabs, parts, block, loads, *refs[:3], *held, *refs[3 + ARRAYS : -ARRAYS]),
         pltpu.VMEM((rows, block), bf16),
         pltpu.VMEM((rows, block), bf16),
-        pltpu.VMEM((paths * part, block), bf16),
-        pltpu.VMEM((breadth, total), bf16),
+        pltpu.VMEM((paths * part, total), bf16),
+        pltpu.VMEM((2, breadth, block), bf16),
+        pltpu.VMEM((3 * part, block), bf16),
         pltpu.VMEM((rows, atoms), bf16),
-        pltpu.VMEM((rows, 2 * refs[4].shape[1]), bf16),
+        pltpu.VMEM((rows, 2 * halo_ref.shape[1]), bf16),
         pltpu.VMEM((2, part, atoms), bf16),
         pltpu.VMEM((3 * part, breadth), bf16),
         pltpu.VMEM((atoms, LANES), bf16),
@@ -222,7 +238,7 @@
     slabs,
     parts,
     block,
-    wide,
+    loads,
     live_ref,
     count_ref,
     energy_ref,
@@ -246,6 +262,8 @@
     acc_ref,
     basis_ref,
     geo_ref,
+    dense_ref,
+    flat_ref,
     agg_ref,
     all_ref,
     send_ref,
@@ -265,6 +283,7 @@
     source_ref,
     weight_ref,
     hidden_ref,
+    lead_ref,
     table_ref,
     halo_table_ref,
     first_table_ref,
@@ -275,6 +294,12 @@
     chans, atoms = state_ref.shape[1:]
     inner_total = inner_edges_ref.shape[1]
     held = halo_ref.shape[1]
+    orders = radial_in_ref.shape[1]
+    sub = min(SUB, block)
+    for load in loads:
+        load.start()
+    for load in loads[:2]:
+        load.wait()
     greet(others("chan", parts) + others("slab", slabs))
 
     values = jnp.broadcast_to(species_ref[...].astype(f32), (16, atoms)).astype(bf16)
@@ -282,117 +307,163 @@
         kind_send_ref[side] = dot(values, onehot_rows(halo_ref[side : side + 1], atoms))[0:8]
     kind_copies = send_halo(kind_send_ref, kind_land_ref, kind_send, kind_recv, slabs)
 
+    for load in loads[2:]:
+        load.wait()
     number_ref[...] = number_rows(atoms)
     start = initial(embed_ref, species_ref[...])
     first_table_ref[0] = dot(mix_ref[0, 0], start.astype(bf16)).astype(bf16)
     for k, path in enumerate((0, 3, 7)):
         paths_ref[k * part : (k + 1) * part] = radial_out_ref[0, path]
     acc_ref[...] = jnp.zeros_like(acc_ref)
-    entry = turned(radial_in_ref[0])
     lists = (
         (inner_edges_ref, inner_vec_ref, 0, live_ref[0, 0]),
         (outer_edges_ref, outer_vec_ref, inner_total, live_ref[0, 1]),
     )
 
-    def scatter(edges_ref, span, offset, live):
-        lanes = lax.broadcasted_iota(jnp.int32, (1, block), 1) + offset
-        target = jnp.where(lanes < live, edges_ref[1:2, span], -1)
-        acc_ref[...] += dot_nt(mess_ref[...], onehot_tiles(target, number_ref))
-
-    def first(which, step):
-        edges_ref, vec_ref, base, live = lists[which]
-        offset = pl.multiple_of(step * block, block)
-        span = pl.ds(offset, block)
-        place = pl.ds(pl.multiple_of(base + step * block, block), block)
-        gathered = dot(first_table_ref[which], onehot_tiles(edges_ref[0:1, span], number_ref))
-        squared, inverse, x, y, z = unit(vec_ref[:, span])
-        basis = bessel_rows(squared, inverse, radial_in_ref.shape[1]).astype(bf16)
-        basis_ref[:, place] = basis
-        rows = [x, y, z] + harmonics(x, y, z)
-        geo_ref[:, place] = jnp.concatenate(rows, axis=0)
-        weights = dot(paths_ref[...], radial(entry, radial_mid_ref[0], basis))
-        for lane in range(0, block, LANES):
-            cols = slice(lane, lane + LANES)
-            around = [tall(row[:, cols]) for row in rows]
-            for low in range(0, part, TALL):
-
-                def lead(k):
-                    at = slice(k * part + low, k * part + low + TALL)
-                    return (weights[at, cols] * gathered[low : low + TALL, cols]).astype(bf16)
-
-                def put(k, value):
-                    mess_ref[k * part + low : k * part + low + TALL, cols] = value
-
-                put(0, lead(0))
-                for k, (low_k, high_k) in enumerate(GROUPS[1:]):
-                    value = lead(1 + k)
-                    for j in range(low_k, high_k):
-                        put(j, value * around[j - 1])
-        scatter(edges_ref, span, offset, live)
-
-    def second(which, step):
+    def geometry(which):
+        _, vec_ref, base, _ = lists[which]
+        chunk = 8 * LANES
+        many = math.gcd(4, vec_ref.shape[1] // chunk)
+
+        def body(step, carry):
+            for part in range(many):
+                piece(step * many + part, dense_ref.at[part], flat_ref.at[part])
+            return carry
+
+        def piece(step, dense_ref, flat_ref):
+            offset = pl.multiple_of(step * chunk, chunk)
+            for j in range(8):
+                cols = pl.ds(pl.multiple_of(offset + j * LANES, LANES), LANES)
+                for axis in range(3):
+                    dense_ref[axis * 8 + j : axis * 8 + j + 1] = vec_ref[axis : axis + 1, cols]
+            squared, inverse, x, y, z = unit([dense_ref[8 * axis : 8 * axis + 8] for axis in range(3)])
+            rows = bessel_rows(squared, inverse, orders) + [x, y, z] + harmonics(x, y, z)
+            for k, row in enumerate(rows):
+                flat_ref[8 * k : 8 * k + 8] = row
+            for j in range(8):
+                cols = pl.ds(pl.multiple_of(base + offset + j * LANES, LANES), LANES)
+                basis_ref[:, cols] = flat_ref[pl.ds(j, orders, stride=8)].astype(bf16)
+                geo_ref[:, cols] = flat_ref[pl.ds(8 * orders + j, 8, stride=8)]
+
+        lax.fori_loop(0, vec_ref.shape[1] // (many * chunk), body, 0)
+
+    def hidden(layer, entry, place):
+        hidden_ref[0] = silu(dot(entry, basis_ref[:, place])).astype(bf16)
+        hidden_ref[1] = silu(dot(radial_mid_ref[layer], hidden_ref[0])).astype(bf16)
+
+    def sweep(make, which):
         edges_ref, _, base, live = lists[which]
-        offset = pl.multiple_of(step * block, block)
-        span = pl.ds(offset, block)
-        place = pl.ds(pl.multiple_of(base + step * block, block), block)
+
+        def body(step, carry):
+            offset = step * block
+
+            def span(j):
+                return pl.ds(pl.multiple_of(offset + j * sub, sub), sub)
+
+            def place(j):
+                return pl.ds(pl.multiple_of(base + offset + j * sub, sub), sub)
+
+            def scatter(j):
+                lanes = lax.broadcasted_iota(jnp.int32, (1, sub), 1) + (offset + j * sub)
+                target = jnp.where(lanes < live, edges_ref[1:2, span(j)], -1)
+                acc_ref[...] += dot_nt(mess_ref[:, j * sub : (j + 1) * sub], onehot_tiles(target, number_ref))
+
+            def gather(j, features):
+                return dot(features, onehot_tiles(edges_ref[0:1, span(j)], number_ref)).astype(bf16)
+
+            make(which, pl.ds(pl.multiple_of(base + offset, block), block), place, gather, scatter)
+            return carry
+
+        lax.fori_loop(0, edges_ref.shape[1] // block, body, 0)
+
+    entry = turned(radial_in_ref[0])
+
+    def first(which, whole, place, gather, scatter):
+        hidden(0, entry, whole)
+        for j in range(block // sub):
+            source_ref[0:part, j * sub : (j + 1) * sub] = gather(j, first_table_ref[which])
+        lead_ref[...] = dot(paths_ref[...], hidden_ref[1]).astype(bf16)
+
+        def combine(j):
+            geo = geo_ref[:, place(j)]
+            for lane in range(0, sub, LANES):
+                cols = slice(j * sub + lane, j * sub + lane + LANES)
+                around = [tall(geo[k : k + 1, lane : lane + LANES]) for k in range(8)]
+                for low in range(0, part, TALL):
+                    held = source_ref[low : low + TALL, cols]
+
+                    def lead(k):
+                        return lead_ref[k * part + low : k * part + low + TALL, cols] * held
+
+                    def put(k, value):
+                        mess_ref[k * part + low : k * part + low + TALL, cols] = value
+
+                    put(0, lead(0))
+                    for k, (low_k, high_k) in enumerate(GROUPS[1:]):
+                        value = lead(1 + k)
+                        for i in range(low_k, high_k):
+                            put(i, value * around[i - 1])
+
+        staged([combine, scatter], block // sub)
+
+    def second(which, whole, place, gather, scatter):
         features_ref = (table_ref, halo_table_ref)[which]
-        source_ref[...] = dot(features_ref[...], onehot_tiles(edges_ref[0:1, span], number_ref)).astype(bf16)
-        weight_ref[...] = dot(radial_out, hidden_ref[:, place]).astype(bf16)
-        geo = geo_ref[:, place]
-        for lane in range(0, block, LANES):
-            cols = slice(lane, lane + LANES)
-            rows = [geo[k : k + 1, cols] for k in range(8)]
-            x, y, z, *q = [tall(row) for row in rows]
-            hx, hy, hz = [tall(half_root * row) for row in rows[:3]]
-            for low in range(0, part, TALL):
-
-                def at(ref, k):
-                    return ref[k * part + low : k * part + low + TALL, cols]
-
-                def put(k, value):
-                    mess_ref[k * part + low : k * part + low + TALL, cols] = value
-
-                s = at(source_ref, 0)
-                v = [at(source_ref, k) for k in (1, 2, 3)]
-                t = [at(source_ref, k) for k in (4, 5, 6, 7, 8)]
-                along = v[0] * x + v[1] * y + v[2] * z
-                tq = t[0] * q[0] + t[1] * q[1] + t[2] * q[2] + t[3] * q[3] + t[4] * q[4]
-                put(0, at(weight_ref, 0) * s + at(weight_ref, 1) * tq + at(weight_ref, 2) * along)
-                ws = at(weight_ref, 3) * s
-                w4, w5, w6 = at(weight_ref, 4), at(weight_ref, 5), at(weight_ref, 6)
-                cross = [
-                    v[1] * z - v[2] * y,
-                    v[2] * x - v[0] * z,
-                    v[0] * y - v[1] * x,
-                ]
-                t3 = 0.5 * t[2]
-                grad = [
-                    hy * t[0] - x * t3 + hz * t[3] + hx * t[4],
-                    hx * t[0] + hz * t[1] - y * t3 - hy * t[4],
-                    hy * t[1] + z * t[2] + hx * t[3],
-                ]
-                for k, side in enumerate((x, y, z)):
-                    put(1 + k, ws * side + w4 * v[k] + w5 * cross[k] + w6 * grad[k])
-                ws = at(weight_ref, 7) * s
-                w8, w9 = at(weight_ref, 8), at(weight_ref, 9)
-                sym = [
-                    hy * v[0] + hx * v[1],
-                    hz * v[1] + hy * v[2],
-                    1.5 * v[2] * z - 0.5 * along,
-                    hz * v[0] + hx * v[2],
-                    hx * v[0] - hy * v[1],
-                ]
-                for k in range(5):
-                    put(4 + k, ws * q[k] + w8 * t[k] + w9 * sym[k])
-        scatter(edges_ref, span, offset, live)
-
-    def sweep(visit, which):
-        def body(step, carry):
-            visit(which, step)
-            return carry
-
-        lax.fori_loop(0, lists[which][0].shape[1] // block, body, 0)
-
+
+        def fetch(j):
+            source_ref[:, j * sub : (j + 1) * sub] = gather(j, features_ref[...])
+
+        def combine(j):
+            geo = geo_ref[:, place(j)]
+            for lane in range(0, sub, LANES):
+                cols = slice(j * sub + lane, j * sub + lane + LANES)
+                x, y, z, *q = [tall(geo[k : k + 1, lane : lane + LANES]) for k in range(8)]
+                weighed = pl.ds(pl.multiple_of(place(j).start + lane, LANES), LANES)
+                for low in range(0, part, TALL):
+
+                    def at(k):
+                        return source_ref[k * part + low : k * part + low + TALL, cols]
+
+                    def path(k):
+                        return weight_ref[k * part + low : k * part + low + TALL, weighed]
+
+                    def put(k, value):
+                        mess_ref[k * part + low : k * part + low + TALL, cols] = value
+
+                    s = at(0)
+                    v = [at(k) for k in (1, 2, 3)]
+                    t = [at(k) for k in (4, 5, 6, 7, 8)]
+                    a, b, c = v[0] * x, v[1] * y, v[2] * z
+                    flat = a + b
+                    along = flat + c
+                    pairs = [
+                        (v[1] * z, v[2] * y),
+                        (v[2] * x, v[0] * z),
+                        (v[0] * y, v[1] * x),
+                    ]
+                    third = root_third * t[2]
+                    grad = [
+                        y * t[0] + z * t[3] + x * (t[4] - third),
+                        x * t[0] + z * t[1] - y * (t[4] + third),
+                        y * t[1] + x * t[3] + z * (third + third),
+                    ]
+                    tq = x * grad[0] + y * grad[1] + z * grad[2]
+                    put(0, path(0) * s + path(1) * tq + path(2) * along)
+                    ws = path(3) * s
+                    w4, w5, w6 = path(4), path(5), path(6)
+                    for k, side in enumerate((x, y, z)):
+                        one, two = pairs[k]
+                        put(1 + k, ws * side + w4 * v[k] + w5 * (one - two) + w6 * grad[k])
+                    ws = path(7) * s
+                    w8, w9 = path(8), path(9)
+                    sums = [one + two for one, two in pairs]
+                    sym = [sums[2], sums[0], (2.0 * root_third) * c - root_third * flat, sums[1], a - b]
+                    for k in range(5):
+                        put(4 + k, ws * q[k] + w8 * t[k] + w9 * sym[k])
+
+        staged([fetch, combine, scatter], block // sub)
+
+    geometry(0)
+    geometry(1)
     sweep(first, 0)
     for copy in kind_copies:
         copy.wait()
@@ -403,13 +474,19 @@
     copies, component = exchange(agg_ref.at[0], all_ref.at[0], agg_send.at[0], agg_recv.at[0], parts)
     acc_ref[...] = jnp.zeros_like(acc_ref)
     entry_next = turned(radial_in_ref[1])
+    paths = radial_out_ref.shape[1]
 
     def prepare(step, carry):
-        span = pl.ds(pl.multiple_of(step * wide, wide), wide)
-        hidden_ref[:, span] = radial(entry_next, radial_mid_ref[1], basis_ref[:, span])
+        whole = pl.ds(pl.multiple_of(step * block, block), block)
+        hidden(1, entry_next, whole)
+        for path in range(paths):
+            weighed = dot(radial_out_ref[1, path], hidden_ref[1])
+            if path in (1, 6, 9):
+                weighed = weighed * half_root
+            weight_ref[path * part : (path + 1) * part, whole] = weighed.astype(bf16)
         return carry
 
-    lax.fori_loop(0, basis_ref.shape[1] // wide, prepare, 0)
+    lax.fori_loop(0, basis_ref.shape[1] // block, prepare, 0)
     picks = jnp.concatenate([onehot_rows(halo_ref[side : side + 1], atoms) for side in range(2)], axis=1)
     outs = Updates(component, turned(scalar_ref[0]), irrep_ref, 0)
     for k in range(9):
@@ -418,18 +495,14 @@
             out += start
         state_ref[k] = out
         which = 0 if k == 0 else (1 if k < 4 else 2)
-        span = slice(k * part, (k + 1) * part)
-        mixed = dot(mix_ref[1, which], out.astype(bf16)).astype(bf16)
-        table_ref[span] = mixed
-        picked = dot(mixed, picks).astype(bf16)
-        for side in range(2):
-            send_ref[side, span] = picked[:, side * held : (side + 1) * held]
+        table_ref[k * part : (k + 1) * part] = dot(mix_ref[1, which], out.astype(bf16)).astype(bf16)
+    picked = dot(table_ref[...], picks).astype(bf16)
+    for side in range(2):
+        send_ref[side] = picked[:, side * held : (side + 1) * held]
     for copy in copies:
         copy.wait_send()
     halo_copies = send_halo(send_ref, land_ref, halo_send, halo_recv, slabs)
 
-    paths, _, breadth = radial_out_ref.shape[1:]
-    radial_out = radial_out_ref[1].reshape(paths * part, breadth)
     sweep(second, 0)
     for copy in halo_copies:
         copy.wait()
@@ -449,7 +522,7 @@
     out = state_ref[0] + outs[0]
     state_ref[0] = out
     total = jnp.sum(out * readout, axis=0, keepdims=True) + own
-    total = jnp.where(lanes < count_ref[0], total, 0.0)
+    total = jnp.where(lanes < count_ref[0, 0], total, 0.0)
     me = lax.axis_index("slab")
     energies_ref[me] = jnp.broadcast_to(jnp.sum(total, axis=1, keepdims=True), energies_ref.shape[1:])
     atom_ref[...] = total
@@ -466,6 +539,12 @@
     for copy in sums:
         copy.wait()
     mean_ref[...] = jnp.sum(energies_ref[...], axis=0)[0:1, 0:1] * (1.0 / (atoms * slabs))
+
+
+def deliver(state_in_ref, atom_in_ref, mean_in_ref, state_ref, atom_ref, mean_ref):
+    state_ref[...] = state_in_ref[...]
+    atom_ref[...] = atom_in_ref[...]
+    mean_ref[...] = mean_in_ref[...]
 
 
 vmem = pl.BlockSpec(memory_space=pltpu.VMEM)
@@ -504,21 +583,39 @@
     total = inner_total + outer_total
     shared = math.gcd(inner_total, outer_total)
     block = math.gcd(BLOCK, shared)
-    wide = math.gcd(WIDE, shared)
     dma = pltpu.SemaphoreType.DMA
-    node_state, atom_energy, mean_energy = pl.pallas_call(
-        functools.partial(kernel, slabs, parts, block, wide),
-        out_shape=(
-            jax.ShapeDtypeStruct((9, chans, atoms), f32),
-            jax.ShapeDtypeStruct((1, atoms), f32),
-            jax.ShapeDtypeStruct((1, 1), f32),
-        ),
-        in_specs=[smem] * 3 + [vmem] * 14,
+    arrays = (
+        species[None, :],
+        halo,
+        inner_edges,
+        outer_edges,
+        inner_vec,
+        outer_vec,
+        embed_table.T,
+        jnp.swapaxes(radial_in, 1, 2),
+        radial_mid,
+        radial_out,
+        mix_in,
+        jnp.swapaxes(mix_scalar, 1, 2),
+        mix_irrep,
+        readout[None, :],
+    )
+    shapes = (
+        jax.ShapeDtypeStruct((9, chans, atoms), f32),
+        jax.ShapeDtypeStruct((1, atoms), f32),
+        jax.ShapeDtypeStruct((1, 1), f32),
+    )
+    results = pl.pallas_call(
+        functools.partial(kernel, slabs, parts, block),
+        out_shape=shapes,
+        in_specs=[smem] * 3 + [pl.BlockSpec(memory_space=pltpu.HBM)] * ARRAYS,
         out_specs=(vmem, vmem, vmem),
         scratch_shapes=[
             pltpu.VMEM((rows, atoms), f32),
             pltpu.VMEM((basis, total), bf16),
             pltpu.VMEM((8, total), f32),
+            pltpu.VMEM((4, 24, LANES), f32),
+            pltpu.VMEM((4, 8 * (basis + 8), LANES), f32),
             pltpu.VMEM((2, rows, atoms), bf16),
             pltpu.VMEM((2, parts, rows, atoms), bf16),
             pltpu.VMEM((2, rows, held), bf16),
@@ -534,6 +631,8 @@
             dma((2,)),
             dma((slabs - 1,)),
             dma((slabs - 1,)),
+            *[pltpu.VMEM(array.shape, array.dtype) for array in arrays],
+            dma((ARRAYS,)),
         ],
         compiler_params=pltpu.CompilerParams(
             vmem_limit_bytes=60 * 1024 * 1024, collective_id=0, has_side_effects=True
@@ -541,23 +640,18 @@
         name="message_passing",
     )(
         edge_count,
-        atom_count,
+        atom_count[None, :],
         species_energy,
-        species[None, :],
-        halo,
-        inner_edges,
-        outer_edges,
-        inner_vec,
-        outer_vec,
-        embed_table.T,
-        jnp.swapaxes(radial_in, 1, 2),
-        radial_mid,
-        radial_out,
-        mix_in,
-        jnp.swapaxes(mix_scalar, 1, 2),
-        mix_irrep,
-        readout[None, :],
+        *arrays,
     )
+    node_state, atom_energy, mean_energy = pl.pallas_call(
+        deliver,
+        out_shape=shapes,
+        in_specs=[vmem] * 3,
+        out_specs=(vmem,) * 3,
+        compiler_params=pltpu.CompilerParams(vmem_limit_bytes=8 * 1024 * 1024),
+        name="deliver",
+    )(*results)
     return (node_state, atom_energy[0], mean_energy[0, 0])
 
 

time: 47.6 us -> 43.1 us (0.905)
  Pallas kernels: 41.9 us -> 39.9 us
  between operations: 3 us -> 1.3 us
  local copies, waits for them, and re-layouts: 2.48 us -> 1.67 us
    pallas_call x1 -> x2, Pallas kernels: 41.9 us -> 39.9 us  [the longest x1 38.4 us: local(): pl.pallas_call(functools.partial(kernel, slabs, parts, block), out_shape=...]
    unnamed x4, local copies, waits for them, and re-layouts: 2.48 us -> 1.67 us
where the time goes in v2:
time: 43.1 us; the launch traced here: 42.9 us
  Pallas kernels  39.9 us (93%)
  local copies, waits for them, and re-layouts  1.67 us (4%)
  between operations  1.3 us (3%)
    pallas_call x1, Pallas kernels, local(): pl.pallas_call(functools.partial(kernel, slabs, parts, block), out_shape=...  38.4 us
    unnamed x4, local copies, waits for them, and re-layouts  1.67 us
    pallas_call x1, Pallas kernels, local(): pl.pallas_call(deliver, out_shape=shapes, in_specs=[vmem] * 3, out_specs=...  1.48 us

profile of v2, /device:TPU:0, one launch (start us, length us, event | category | flops | bytes accessed | tf_op | source)
XLA Modules:
  0.0 42.9 jit_solution(3924391335695879591)
XLA Ops:
  1.3 38.4 %message_passing.1 = (f32[9,64,256]{2,1,0:T(8,128)}, f32[1,256]{1,0:T(1,128)}, f32[1,1]{1,0:T(1,128)}) custom-call(s32[1,2]{1,0:T(1,128)} %refs_0_.1, s32[1,1]{1,0:T(1,128)} %bitcast.9.refs_1_, f32[5]{0:T(128)} %refs_2_.1, s32[1,256]{1,0:T(1,128)} %bitcast.13, s32[2,128]{1,0:T(2,128)} %bitcast.14, s32[2,12288]{1,0:T(2,128)} %refs_5_.1, s32[2,4096]{1,0:T(2,128)} %refs_6_.1, ...), custom_call_target="tpu_custom_call" | custom-call | tf_op jit(solution)/shard_map/message_passing/pallas_call | solution.py:608
  39.7 0.0 copy-start.1
  39.7 0.6 %copy-done.1 = f32[1,256]{1,0:T(1,128)S(1)} copy-done((f32[1,256]{1,0:T(1,128)S(1)}, f32[1,256]{1,0:T(1,128)}, u32[]{:S(2)}) %copy-start.1) | copy-done | bytes 1048
  40.4 0.0 copy-start
  40.4 1.1 %copy-done = f32[9,64,256]{2,1,0:T(8,128)S(1)} copy-done((f32[9,64,256]{2,1,0:T(8,128)S(1)}, f32[9,64,256]{2,1,0:T(8,128)}, u32[]{:S(2)}) %copy-start) | copy-done | bytes 589848
  41.4 1.5 %deliver.1 = (f32[9,64,256]{2,1,0:T(8,128)}, f32[1,256]{1,0:T(1,128)}, f32[1,1]{1,0:T(1,128)}) custom-call(f32[9,64,256]{2,1,0:T(8,128)S(1)} %copy-done, f32[1,256]{1,0:T(1,128)S(1)} %copy-done.1, f32[1,1]{1,0:T(1,128)} %get-tuple-element.11.mean_in_ref), custom_call_target="tpu_custom_call" | custom-call | tf_op jit(solution)/shard_map/deliver/pallas_call | solution.py:647
Async XLA Ops:
  39.7 0.6 %copy-start.1 = (f32[1,256]{1,0:T(1,128)S(1)}, f32[1,256]{1,0:T(1,128)}, u32[]{:S(2)}) copy-start(f32[1,256]{1,0:T(1,128)} %get-tuple-element.10.atom_in_ref) | copy-start | bytes 3076
  40.4 1.1 %copy-start = (f32[9,64,256]{2,1,0:T(8,128)S(1)}, f32[9,64,256]{2,1,0:T(8,128)}, u32[]{:S(2)}) copy-start(f32[9,64,256]{2,1,0:T(8,128)} %get-tuple-element.9.state_in_ref) | copy-start | bytes 1769476

commit v3 on v2

--- a/solution.py
+++ b/solution.py
@@ -180,6 +180,16 @@
     return copies, component
 
 
+def settled(all_ref):
+    part = all_ref.shape[1] // 9
+
+    def component(k):
+        span = slice(k * part, (k + 1) * part)
+        return jnp.concatenate([all_ref[i, span] for i in range(all_ref.shape[0])], axis=0)
+
+    return component
+
+
 class Updates:
     def __init__(self, component, scalar, irrep_ref, layer):
         self.component, self.layer, self.irrep = component, layer, irrep_ref
@@ -225,7 +235,8 @@
         pltpu.VMEM((rows, block), bf16),
         pltpu.VMEM((paths * part, total), bf16),
         pltpu.VMEM((2, breadth, block), bf16),
-        pltpu.VMEM((3 * part, block), bf16),
+        pltpu.VMEM((2, 3 * part, block), bf16),
+        pltpu.VMEM((2, part, block), bf16),
         pltpu.VMEM((rows, atoms), bf16),
         pltpu.VMEM((rows, 2 * halo_ref.shape[1]), bf16),
         pltpu.VMEM((2, part, atoms), bf16),
@@ -256,10 +267,13 @@
     scalar_ref,
     irrep_ref,
     readout_ref,
-    state_ref,
+    state_out_ref,
     atom_ref,
     mean_ref,
+    state_ref,
+    state_sem,
     acc_ref,
+    other_ref,
     basis_ref,
     geo_ref,
     dense_ref,
@@ -284,6 +298,7 @@
     weight_ref,
     hidden_ref,
     lead_ref,
+    origin_ref,
     table_ref,
     halo_table_ref,
     first_table_ref,
@@ -307,14 +322,9 @@
         kind_send_ref[side] = dot(values, onehot_rows(halo_ref[side : side + 1], atoms))[0:8]
     kind_copies = send_halo(kind_send_ref, kind_land_ref, kind_send, kind_recv, slabs)
 
-    for load in loads[2:]:
-        load.wait()
     number_ref[...] = number_rows(atoms)
-    start = initial(embed_ref, species_ref[...])
-    first_table_ref[0] = dot(mix_ref[0, 0], start.astype(bf16)).astype(bf16)
-    for k, path in enumerate((0, 3, 7)):
-        paths_ref[k * part : (k + 1) * part] = radial_out_ref[0, path]
     acc_ref[...] = jnp.zeros_like(acc_ref)
+    other_ref[...] = jnp.zeros_like(other_ref)
     lists = (
         (inner_edges_ref, inner_vec_ref, 0, live_ref[0, 0]),
         (outer_edges_ref, outer_vec_ref, inner_total, live_ref[0, 1]),
@@ -351,73 +361,83 @@
         hidden_ref[0] = silu(dot(entry, basis_ref[:, place])).astype(bf16)
         hidden_ref[1] = silu(dot(radial_mid_ref[layer], hidden_ref[0])).astype(bf16)
 
-    def sweep(make, which):
-        edges_ref, _, base, live = lists[which]
-
-        def body(step, carry):
-            offset = step * block
-
-            def span(j):
-                return pl.ds(pl.multiple_of(offset + j * sub, sub), sub)
-
-            def place(j):
-                return pl.ds(pl.multiple_of(base + offset + j * sub, sub), sub)
-
-            def scatter(j):
-                lanes = lax.broadcasted_iota(jnp.int32, (1, sub), 1) + (offset + j * sub)
-                target = jnp.where(lanes < live, edges_ref[1:2, span(j)], -1)
-                acc_ref[...] += dot_nt(mess_ref[:, j * sub : (j + 1) * sub], onehot_tiles(target, number_ref))
-
-            def gather(j, features):
-                return dot(features, onehot_tiles(edges_ref[0:1, span(j)], number_ref)).astype(bf16)
-
-            make(which, pl.ds(pl.multiple_of(base + offset, block), block), place, gather, scatter)
-            return carry
-
-        lax.fori_loop(0, edges_ref.shape[1] // block, body, 0)
-
-    entry = turned(radial_in_ref[0])
-
-    def first(which, whole, place, gather, scatter):
-        hidden(0, entry, whole)
-        for j in range(block // sub):
-            source_ref[0:part, j * sub : (j + 1) * sub] = gather(j, first_table_ref[which])
-        lead_ref[...] = dot(paths_ref[...], hidden_ref[1]).astype(bf16)
-
-        def combine(j):
-            geo = geo_ref[:, place(j)]
-            for lane in range(0, sub, LANES):
-                cols = slice(j * sub + lane, j * sub + lane + LANES)
-                around = [tall(geo[k : k + 1, lane : lane + LANES]) for k in range(8)]
-                for low in range(0, part, TALL):
-                    held = source_ref[low : low + TALL, cols]
-
-                    def lead(k):
-                        return lead_ref[k * part + low : k * part + low + TALL, cols] * held
-
-                    def put(k, value):
-                        mess_ref[k * part + low : k * part + low + TALL, cols] = value
-
-                    put(0, lead(0))
-                    for k, (low_k, high_k) in enumerate(GROUPS[1:]):
-                        value = lead(1 + k)
-                        for i in range(low_k, high_k):
-                            put(i, value * around[i - 1])
-
-        staged([combine, scatter], block // sub)
-
-    def second(which, whole, place, gather, scatter):
+    subs = block // sub
+
+    def scatter(which, step, j, into):
+        edges_ref, _, _, live = lists[which]
+        offset = step * block + j * sub
+        lanes = lax.broadcasted_iota(jnp.int32, (1, sub), 1) + offset
+        target = jnp.where(lanes < live, edges_ref[1:2, offset : offset + sub], -1)
+        into[...] += dot_nt(mess_ref[:, j * sub : (j + 1) * sub], onehot_tiles(target, number_ref))
+
+    def gather(which, step, j, features):
+        offset = step * block + j * sub
+        edges_ref = lists[which][0]
+        return dot(features, onehot_tiles(edges_ref[0:1, offset : offset + sub], number_ref)).astype(bf16)
+
+    def blocks(which):
+        return [(which, step) for step in range(lists[which][0].shape[1] // block)]
+
+    def first(now, then):
+        halves = (range(subs // 2), range(subs // 2, subs))
+        if then is not None:
+            which, step = then
+            slot = (lists[which][2] // block + step) % 2
+            base = lists[which][2] + step * block
+            hidden_ref[0] = silu(dot(entry, basis_ref[:, base : base + block])).astype(bf16)
+        for half in range(2):
+            if now is not None:
+                for j in halves[half]:
+                    combine_first(*now, j)
+                    scatter(*now, j, (acc_ref, other_ref)[j % 2])
+            if then is not None and half == 0:
+                hidden_ref[1] = silu(dot(radial_mid_ref[0], hidden_ref[0])).astype(bf16)
+        if then is not None:
+            for j in range(subs):
+                origin_ref[slot, :, j * sub : (j + 1) * sub] = gather(which, step, j, first_table_ref[which])
+            lead_ref[slot] = dot(paths_ref[...], hidden_ref[1]).astype(bf16)
+
+    def combine_first(which, step, j):
+        start = lists[which][2] + step * block + j * sub
+        slot = (lists[which][2] // block + step) % 2
+        geo = geo_ref[:, start : start + sub]
+        for lane in range(0, sub, LANES):
+            cols = slice(j * sub + lane, j * sub + lane + LANES)
+            around = [tall(geo[k : k + 1, lane : lane + LANES]) for k in range(8)]
+            for low in range(0, part, TALL):
+                held = origin_ref[slot, low : low + TALL, cols]
+
+                def lead(k):
+                    return lead_ref[slot, k * part + low : k * part + low + TALL, cols] * held
+
+                def put(k, value):
+                    mess_ref[k * part + low : k * part + low + TALL, cols] = value
+
+                put(0, lead(0))
+                for k, (low_k, high_k) in enumerate(GROUPS[1:]):
+                    value = lead(1 + k)
+                    for i in range(low_k, high_k):
+                        put(i, value * around[i - 1])
+
+    def second(which):
         features_ref = (table_ref, halo_table_ref)[which]
 
-        def fetch(j):
-            source_ref[:, j * sub : (j + 1) * sub] = gather(j, features_ref[...])
-
-        def combine(j):
-            geo = geo_ref[:, place(j)]
+        def fetch(i):
+            step, j = divmod(i, subs)
+            source_ref[:, j * sub : (j + 1) * sub] = gather(which, step, j, features_ref[...])
+
+        def settle(i):
+            step, j = divmod(i, subs)
+            scatter(which, step, j, acc_ref)
+
+        def combine(i):
+            step, j = divmod(i, subs)
+            start = lists[which][2] + step * block + j * sub
+            geo = geo_ref[:, start : start + sub]
             for lane in range(0, sub, LANES):
                 cols = slice(j * sub + lane, j * sub + lane + LANES)
                 x, y, z, *q = [tall(geo[k : k + 1, lane : lane + LANES]) for k in range(8)]
-                weighed = pl.ds(pl.multiple_of(place(j).start + lane, LANES), LANES)
+                weighed = slice(start + lane, start + lane + LANES)
                 for low in range(0, part, TALL):
 
                     def at(k):
@@ -460,20 +480,35 @@
                     for k in range(5):
                         put(4 + k, ws * q[k] + w8 * t[k] + w9 * sym[k])
 
-        staged([fetch, combine, scatter], block // sub)
-
+        staged([fetch, combine, settle], len(blocks(which)) * subs)
+
+    for load in loads[4:6]:
+        load.wait()
     geometry(0)
     geometry(1)
-    sweep(first, 0)
-    for copy in kind_copies:
-        copy.wait()
-    kinds = jnp.concatenate([kind_land_ref[0, 0:1], kind_land_ref[1, 0:1]], axis=1).astype(jnp.int32)
-    first_table_ref[1] = dot(mix_ref[0, 0], initial(embed_ref, kinds).astype(bf16)).astype(bf16)
-    sweep(first, 1)
-    agg_ref[0] = (acc_ref[...] * neighbour_norm).astype(bf16)
+    for i, load in enumerate(loads):
+        if i not in (0, 1, 4, 5):
+            load.wait()
+    start = initial(embed_ref, species_ref[...])
+    first_table_ref[0] = dot(mix_ref[0, 0], start.astype(bf16)).astype(bf16)
+    for k, path in enumerate((0, 3, 7)):
+        paths_ref[k * part : (k + 1) * part] = radial_out_ref[0, path]
+    entry = turned(radial_in_ref[0])
+    entry_next = turned(radial_in_ref[1])
+    mixers = [turned(scalar_ref[layer]) for layer in range(2)]
+    order = blocks(0) + blocks(1)
+    met = len(blocks(0)) - 1
+    first(None, order[0])
+    for i, (now, then) in enumerate(zip(order, order[1:] + [None])):
+        if i == met:
+            for copy in kind_copies:
+                copy.wait()
+            kinds = jnp.concatenate([kind_land_ref[0, 0:1], kind_land_ref[1, 0:1]], axis=1).astype(jnp.int32)
+            first_table_ref[1] = dot(mix_ref[0, 0], initial(embed_ref, kinds).astype(bf16)).astype(bf16)
+        first(now, then)
+    agg_ref[0] = ((acc_ref[...] + other_ref[...]) * neighbour_norm).astype(bf16)
     copies, component = exchange(agg_ref.at[0], all_ref.at[0], agg_send.at[0], agg_recv.at[0], parts)
     acc_ref[...] = jnp.zeros_like(acc_ref)
-    entry_next = turned(radial_in_ref[1])
     paths = radial_out_ref.shape[1]
 
     def prepare(step, carry):
@@ -487,8 +522,10 @@
         return carry
 
     lax.fori_loop(0, basis_ref.shape[1] // block, prepare, 0)
+    for copy in copies:
+        copy.wait_recv()
     picks = jnp.concatenate([onehot_rows(halo_ref[side : side + 1], atoms) for side in range(2)], axis=1)
-    outs = Updates(component, turned(scalar_ref[0]), irrep_ref, 0)
+    outs = Updates(settled(all_ref.at[0]), mixers[0], irrep_ref, 0)
     for k in range(9):
         out = outs[k]
         if k == 0:
@@ -503,12 +540,12 @@
         copy.wait_send()
     halo_copies = send_halo(send_ref, land_ref, halo_send, halo_recv, slabs)
 
-    sweep(second, 0)
+    second(0)
     for copy in halo_copies:
         copy.wait()
     for side in range(2):
         halo_table_ref[:, side * held : (side + 1) * held] = land_ref[side]
-    sweep(second, 1)
+    second(1)
     agg_ref[1] = (acc_ref[...] * neighbour_norm).astype(bf16)
     copies, component = exchange(agg_ref.at[1], all_ref.at[1], agg_send.at[1], agg_recv.at[1], parts)
     lines = lax.broadcasted_iota(jnp.int32, (chans, chans), 0)
@@ -518,7 +555,7 @@
     for kind in range(energy_ref.shape[0]):
         own = jnp.where(species_ref[...] == kind, energy_ref[kind], own)
     lanes = lax.broadcasted_iota(jnp.int32, (1, atoms), 1)
-    outs = Updates(component, turned(scalar_ref[1]), irrep_ref, 1)
+    outs = Updates(component, mixers[1], irrep_ref, 1)
     out = state_ref[0] + outs[0]
     state_ref[0] = out
     total = jnp.sum(out * readout, axis=0, keepdims=True) + own
@@ -532,22 +569,39 @@
     ]
     for copy in sums:
         copy.start()
+    writes = [pltpu.make_async_copy(state_ref.at[k], state_out_ref.at[k], state_sem.at[k]) for k in range(9)]
     for k in range(1, 9):
         state_ref[k] = state_ref[k] + outs[k]
+        if k > 1:
+            writes[k - 2].start()
     for copy in copies:
         copy.wait_send()
+    for write in writes[7:]:
+        write.start()
     for copy in sums:
         copy.wait()
+    for write in writes:
+        write.wait()
     mean_ref[...] = jnp.sum(energies_ref[...], axis=0)[0:1, 0:1] * (1.0 / (atoms * slabs))
 
 
-def deliver(state_in_ref, atom_in_ref, mean_in_ref, state_ref, atom_ref, mean_ref):
-    state_ref[...] = state_in_ref[...]
-    atom_ref[...] = atom_in_ref[...]
-    mean_ref[...] = mean_in_ref[...]
+def deliver(*refs):
+    state_in, atom_in, mean_in, state_out, atom_out, mean_out, state, atom, mean, sems = refs
+    pairs = [(state_in.at[k], state.at[k], state_out.at[k]) for k in range(state.shape[0])]
+    pairs += [(atom_in, atom, atom_out), (mean_in, mean, mean_out)]
+    loads = [pltpu.make_async_copy(a, b, sems.at[0, i]) for i, (a, b, _) in enumerate(pairs)]
+    writes = [pltpu.make_async_copy(b, c, sems.at[1, i]) for i, (_, b, c) in enumerate(pairs)]
+    for load in loads:
+        load.start()
+    for load, write in zip(loads, writes, strict=True):
+        load.wait()
+        write.start()
+    for write in writes:
+        write.wait()
 
 
 vmem = pl.BlockSpec(memory_space=pltpu.VMEM)
+anywhere = pl.BlockSpec(memory_space=pl.ANY)
 smem = pl.BlockSpec(memory_space=pltpu.SMEM)
 
 
@@ -609,8 +663,11 @@
         functools.partial(kernel, slabs, parts, block),
         out_shape=shapes,
         in_specs=[smem] * 3 + [pl.BlockSpec(memory_space=pltpu.HBM)] * ARRAYS,
-        out_specs=(vmem, vmem, vmem),
+        out_specs=(anywhere, vmem, vmem),
         scratch_shapes=[
+            pltpu.VMEM((9, chans, atoms), f32),
+            dma((9,)),
+            pltpu.VMEM((rows, atoms), f32),
             pltpu.VMEM((rows, atoms), f32),
             pltpu.VMEM((basis, total), bf16),
             pltpu.VMEM((8, total), f32),
@@ -647,9 +704,10 @@
     node_state, atom_energy, mean_energy = pl.pallas_call(
         deliver,
         out_shape=shapes,
-        in_specs=[vmem] * 3,
-        out_specs=(vmem,) * 3,
-        compiler_params=pltpu.CompilerParams(vmem_limit_bytes=8 * 1024 * 1024),
+        in_specs=[anywhere] * 3,
+        out_specs=(anywhere,) * 3,
+        scratch_shapes=[pltpu.VMEM(shape.shape, shape.dtype) for shape in shapes] + [dma((2, 11))],
+        compiler_params=pltpu.CompilerParams(vmem_limit_bytes=60 * 1024 * 1024),
         name="deliver",
     )(*results)
     return (node_state, atom_energy[0], mean_energy[0, 0])

time: 43.1 us -> 40.7 us (0.944)
  local copies, waits for them, and re-layouts: 1.67 us -> 0 us
  Pallas kernels: 39.9 us -> 39 us
    pallas_call x1, Pallas kernels: 38.4 us -> 36.5 us  [local(): pl.pallas_call(functools.partial(kernel, slabs, parts, block), out_shape=...]
    unnamed x4 -> x0, local copies, waits for them, and re-layouts: 1.67 us -> none
    pallas_call x1, Pallas kernels: 1.48 us -> 2.49 us  [local(): pl.pallas_call(deliver, out_shape=shapes, in_specs=[anywhere] * 3, out_sp...]
where the time goes in v3:
time: 40.7 us; the launch traced here: 40.5 us
  Pallas kernels  39 us (96%)
  between operations  1.45 us (4%)
    pallas_call x1, Pallas kernels, local(): pl.pallas_call(functools.partial(kernel, slabs, parts, block), out_shape=...  36.5 us
    pallas_call x1, Pallas kernels, local(): pl.pallas_call(deliver, out_shape=shapes, in_specs=[anywhere] * 3, out_sp...  2.49 us

profile of v3, /device:TPU:0, one launch (start us, length us, event | category | flops | bytes accessed | tf_op | source)
XLA Modules:
  0.0 40.5 jit_solution(5310008542288850822)
XLA Ops:
  1.3 36.5 %message_passing.1 = (f32[9,64,256]{2,1,0:T(8,128)}, f32[1,256]{1,0:T(1,128)}, f32[1,1]{1,0:T(1,128)}) custom-call(s32[1,2]{1,0:T(1,128)} %refs_0_.1, s32[1,1]{1,0:T(1,128)} %bitcast.9.refs_1_, f32[5]{0:T(128)} %refs_2_.1, s32[1,256]{1,0:T(1,128)} %bitcast.13, s32[2,128]{1,0:T(2,128)} %bitcast.14, s32[2,12288]{1,0:T(2,128)} %refs_5_.1, s32[2,4096]{1,0:T(2,128)} %refs_6_.1, ...), custom_call_target="tpu_custom_call" | custom-call | tf_op jit(solution)/shard_map/message_passing/pallas_call | solution.py:662
  37.8 2.5 %deliver.1 = (f32[9,64,256]{2,1,0:T(8,128)}, f32[1,256]{1,0:T(1,128)}, f32[1,1]{1,0:T(1,128)}) custom-call(f32[9,64,256]{2,1,0:T(8,128)} %get-tuple-element.9.refs_0_, f32[1,256]{1,0:T(1,128)} %get-tuple-element.10.refs_1_, f32[1,1]{1,0:T(1,128)} %get-tuple-element.11.refs_2_), custom_call_target="tpu_custom_call" | custom-call | tf_op jit(solution)/shard_map/deliver/pallas_call | solution.py:704

commit v4 on v3

--- a/solution.py
+++ b/solution.py
@@ -330,20 +330,15 @@
         (outer_edges_ref, outer_vec_ref, inner_total, live_ref[0, 1]),
     )
 
-    def geometry(which):
+    def geometry(which, block_step):
         _, vec_ref, base, _ = lists[which]
         chunk = 8 * LANES
-        many = math.gcd(4, vec_ref.shape[1] // chunk)
-
-        def body(step, carry):
-            for part in range(many):
-                piece(step * many + part, dense_ref.at[part], flat_ref.at[part])
-            return carry
+        many = block // chunk
 
         def piece(step, dense_ref, flat_ref):
-            offset = pl.multiple_of(step * chunk, chunk)
+            offset = step * chunk
             for j in range(8):
-                cols = pl.ds(pl.multiple_of(offset + j * LANES, LANES), LANES)
+                cols = pl.ds(offset + j * LANES, LANES)
                 for axis in range(3):
                     dense_ref[axis * 8 + j : axis * 8 + j + 1] = vec_ref[axis : axis + 1, cols]
             squared, inverse, x, y, z = unit([dense_ref[8 * axis : 8 * axis + 8] for axis in range(3)])
@@ -351,17 +346,19 @@
             for k, row in enumerate(rows):
                 flat_ref[8 * k : 8 * k + 8] = row
             for j in range(8):
-                cols = pl.ds(pl.multiple_of(base + offset + j * LANES, LANES), LANES)
+                cols = pl.ds(base + offset + j * LANES, LANES)
                 basis_ref[:, cols] = flat_ref[pl.ds(j, orders, stride=8)].astype(bf16)
                 geo_ref[:, cols] = flat_ref[pl.ds(8 * orders + j, 8, stride=8)]
 
-        lax.fori_loop(0, vec_ref.shape[1] // (many * chunk), body, 0)
+        for part in range(many):
+            piece(block_step * many + part, dense_ref.at[part], flat_ref.at[part])
 
     def hidden(layer, entry, place):
         hidden_ref[0] = silu(dot(entry, basis_ref[:, place])).astype(bf16)
         hidden_ref[1] = silu(dot(radial_mid_ref[layer], hidden_ref[0])).astype(bf16)
 
     subs = block // sub
+    paths = radial_out_ref.shape[1]
 
     def scatter(which, step, j, into):
         edges_ref, _, _, live = lists[which]
@@ -378,20 +375,33 @@
     def blocks(which):
         return [(which, step) for step in range(lists[which][0].shape[1] // block)]
 
-    def first(now, then):
+    def weigh(path, place):
+        weighed = dot(radial_out_ref[1, path], hidden_ref[1])
+        if path in (1, 6, 9):
+            weighed = weighed * half_root
+        weight_ref[path * part : (path + 1) * part, place] = weighed.astype(bf16)
+
+    def first(now, then, later):
         halves = (range(subs // 2), range(subs // 2, subs))
         if then is not None:
             which, step = then
             slot = (lists[which][2] // block + step) % 2
             base = lists[which][2] + step * block
             hidden_ref[0] = silu(dot(entry, basis_ref[:, base : base + block])).astype(bf16)
+        else:
+            hidden_ref[0] = silu(dot(entry_next, basis_ref[:, 0:block])).astype(bf16)
+        if later is not None:
+            geometry(*later)
         for half in range(2):
-            if now is not None:
-                for j in halves[half]:
+            for i, j in enumerate(halves[half]):
+                if now is not None:
                     combine_first(*now, j)
                     scatter(*now, j, (acc_ref, other_ref)[j % 2])
-            if then is not None and half == 0:
-                hidden_ref[1] = silu(dot(radial_mid_ref[0], hidden_ref[0])).astype(bf16)
+                if then is None and half == 1:
+                    for path in range(i, paths, len(halves[half])):
+                        weigh(path, slice(0, block))
+            if half == 0:
+                hidden_ref[1] = silu(dot(radial_mid_ref[0 if then else 1], hidden_ref[0])).astype(bf16)
         if then is not None:
             for j in range(subs):
                 origin_ref[slot, :, j * sub : (j + 1) * sub] = gather(which, step, j, first_table_ref[which])
@@ -419,19 +429,22 @@
                     for i in range(low_k, high_k):
                         put(i, value * around[i - 1])
 
-    def second(which):
-        features_ref = (table_ref, halo_table_ref)[which]
+    def second(arrive):
+        order = blocks(0) + blocks(1)
 
         def fetch(i):
-            step, j = divmod(i, subs)
+            (which, step), j = order[i // subs], i % subs
+            if i == len(blocks(0)) * subs:
+                arrive()
+            features_ref = (table_ref, halo_table_ref)[which]
             source_ref[:, j * sub : (j + 1) * sub] = gather(which, step, j, features_ref[...])
 
         def settle(i):
-            step, j = divmod(i, subs)
+            (which, step), j = order[i // subs], i % subs
             scatter(which, step, j, acc_ref)
 
         def combine(i):
-            step, j = divmod(i, subs)
+            (which, step), j = order[i // subs], i % subs
             start = lists[which][2] + step * block + j * sub
             geo = geo_ref[:, start : start + sub]
             for lane in range(0, sub, LANES):
@@ -480,12 +493,11 @@
                     for k in range(5):
                         put(4 + k, ws * q[k] + w8 * t[k] + w9 * sym[k])
 
-        staged([fetch, combine, settle], len(blocks(which)) * subs)
+        staged([fetch, combine, settle], len(order) * subs)
 
     for load in loads[4:6]:
         load.wait()
-    geometry(0)
-    geometry(1)
+    geometry(*(blocks(0) + blocks(1))[0])
     for i, load in enumerate(loads):
         if i not in (0, 1, 4, 5):
             load.wait()
@@ -498,30 +510,26 @@
     mixers = [turned(scalar_ref[layer]) for layer in range(2)]
     order = blocks(0) + blocks(1)
     met = len(blocks(0)) - 1
-    first(None, order[0])
+    first(None, order[0], order[1])
     for i, (now, then) in enumerate(zip(order, order[1:] + [None])):
         if i == met:
             for copy in kind_copies:
                 copy.wait()
             kinds = jnp.concatenate([kind_land_ref[0, 0:1], kind_land_ref[1, 0:1]], axis=1).astype(jnp.int32)
             first_table_ref[1] = dot(mix_ref[0, 0], initial(embed_ref, kinds).astype(bf16)).astype(bf16)
-        first(now, then)
+        first(now, then, order[i + 2] if i + 2 < len(order) else None)
     agg_ref[0] = ((acc_ref[...] + other_ref[...]) * neighbour_norm).astype(bf16)
     copies, component = exchange(agg_ref.at[0], all_ref.at[0], agg_send.at[0], agg_recv.at[0], parts)
     acc_ref[...] = jnp.zeros_like(acc_ref)
-    paths = radial_out_ref.shape[1]
 
     def prepare(step, carry):
         whole = pl.ds(pl.multiple_of(step * block, block), block)
         hidden(1, entry_next, whole)
         for path in range(paths):
-            weighed = dot(radial_out_ref[1, path], hidden_ref[1])
-            if path in (1, 6, 9):
-                weighed = weighed * half_root
-            weight_ref[path * part : (path + 1) * part, whole] = weighed.astype(bf16)
+            weigh(path, whole)
         return carry
 
-    lax.fori_loop(0, basis_ref.shape[1] // block, prepare, 0)
+    lax.fori_loop(1, basis_ref.shape[1] // block, prepare, 0)
     for copy in copies:
         copy.wait_recv()
     picks = jnp.concatenate([onehot_rows(halo_ref[side : side + 1], atoms) for side in range(2)], axis=1)
@@ -540,12 +548,13 @@
         copy.wait_send()
     halo_copies = send_halo(send_ref, land_ref, halo_send, halo_recv, slabs)
 
-    second(0)
-    for copy in halo_copies:
-        copy.wait()
-    for side in range(2):
-        halo_table_ref[:, side * held : (side + 1) * held] = land_ref[side]
-    second(1)
+    def arrive():
+        for copy in halo_copies:
+            copy.wait()
+        for side in range(2):
+            halo_table_ref[:, side * held : (side + 1) * held] = land_ref[side]
+
+    second(arrive)
     agg_ref[1] = (acc_ref[...] * neighbour_norm).astype(bf16)
     copies, component = exchange(agg_ref.at[1], all_ref.at[1], agg_send.at[1], agg_recv.at[1], parts)
     lines = lax.broadcasted_iota(jnp.int32, (chans, chans), 0)
@@ -671,8 +680,8 @@
             pltpu.VMEM((rows, atoms), f32),
             pltpu.VMEM((basis, total), bf16),
             pltpu.VMEM((8, total), f32),
-            pltpu.VMEM((4, 24, LANES), f32),
-            pltpu.VMEM((4, 8 * (basis + 8), LANES), f32),
+            pltpu.VMEM((block // (8 * LANES), 24, LANES), f32),
+            pltpu.VMEM((block // (8 * LANES), 8 * (basis + 8), LANES), f32),
             pltpu.VMEM((2, rows, atoms), bf16),
             pltpu.VMEM((2, parts, rows, atoms), bf16),
             pltpu.VMEM((2, rows, held), bf16),

time: 40.7 us -> 39.8 us (0.978)
  Pallas kernels: 39 us -> 38.2 us
    pallas_call x1, Pallas kernels: 36.5 us -> 35.7 us  [local(): pl.pallas_call(functools.partial(kernel, slabs, parts, block), out_shape=...]
where the time goes in v4:
time: 39.8 us; the launch traced here: 39.6 us
  Pallas kernels  38.2 us (96%)
  between operations  1.45 us (4%)
    pallas_call x1, Pallas kernels, local(): pl.pallas_call(functools.partial(kernel, slabs, parts, block), out_shape=...  35.7 us
    pallas_call x1, Pallas kernels, local(): pl.pallas_call(deliver, out_shape=shapes, in_specs=[anywhere] * 3, out_sp...  2.49 us

profile of v4, /device:TPU:0, one launch (start us, length us, event | category | flops | bytes accessed | tf_op | source)
XLA Modules:
  0.0 39.6 jit_solution(7078642900668429282)
XLA Ops:
  1.3 35.7 %message_passing.1 = (f32[9,64,256]{2,1,0:T(8,128)}, f32[1,256]{1,0:T(1,128)}, f32[1,1]{1,0:T(1,128)}) custom-call(s32[1,2]{1,0:T(1,128)} %refs_0_.1, s32[1,1]{1,0:T(1,128)} %bitcast.9.refs_1_, f32[5]{0:T(128)} %refs_2_.1, s32[1,256]{1,0:T(1,128)} %bitcast.13, s32[2,128]{1,0:T(2,128)} %bitcast.14, s32[2,12288]{1,0:T(2,128)} %refs_5_.1, s32[2,4096]{1,0:T(2,128)} %refs_6_.1, ...), custom_call_target="tpu_custom_call" | custom-call | tf_op jit(solution)/shard_map/message_passing/pallas_call | solution.py:671
  37.0 2.5 %deliver.1 = (f32[9,64,256]{2,1,0:T(8,128)}, f32[1,256]{1,0:T(1,128)}, f32[1,1]{1,0:T(1,128)}) custom-call(f32[9,64,256]{2,1,0:T(8,128)} %get-tuple-element.9.refs_0_, f32[1,256]{1,0:T(1,128)} %get-tuple-element.10.refs_1_, f32[1,1]{1,0:T(1,128)} %get-tuple-element.11.refs_2_), custom_call_target="tpu_custom_call" | custom-call | tf_op jit(solution)/shard_map/deliver/pallas_call | solution.py:713
